TPU v7x, 256 devices: a whole 4x4x8 slice. The times are simulated.
256 devices in a mesh: dp: 64 (over x, z_lo, y, core), sub: 4 (over z_hi).
Axes of the slice: x: 4, y: 4, z: 8 (z_hi: 4, z_lo: 2; z = z_hi * 2 + z_lo), core: 2. Of those that a mesh axis runs over, the one named last changes fastest.
Arguments:
- queries: float32 [16384, 1024], P(('dp', 'sub')), may hold values from -8 to 8
- passages: float32 [16384, 1024], P(('dp', 'sub')), may hold values from -8 to 8
- positives: int32 [16384], P(('dp', 'sub')), may hold values from 0 to 16383, each once
Outputs:
- losses: float32 [16384], P(('dp', 'sub'))
- query_grads: float32 [16384, 1024], P(('dp', 'sub'))
- passage_grads: float32 [16384, 1024], P(('dp', 'sub'))
All inputs are finite; a program needn't handle non-finite values.
Results may differ from a plain program's by a relative error of at most 0.00185.
The roundings to bfloat16 on the way count: a program that leaves them out, or rounds other values in their place, can miss the bound.
Values may be sent and summed in bfloat16 or wider, within the bound.
No kernel may reach another device: no remote copies, remote signals or barrier semaphores. Data moves between devices by JAX's collectives and lax.ppermute only.
A program may use at most 128 MiB of HBM per device.

v0:
```python
import jax
import jax.numpy as jnp
from jax import lax
from jax.sharding import Mesh
from jax.sharding import PartitionSpec as P

DP = ("dp_0", "dp_1", "dp_2", "dp_3")
DP_SUB = ("dp_0", "dp_1", "dp_2", "dp_3", "sub")
logit_scale = 20.0


def laid_out(blocks, dim):
    blocks = jnp.moveaxis(blocks, 0, dim)
    lengths = blocks.shape
    return blocks.reshape(*lengths[:dim], lengths[dim] * lengths[dim + 1], *lengths[dim + 2 :])


def sent_to_all(value, axis):
    devices = lax.axis_size(axis)
    return lax.all_to_all(
        jnp.broadcast_to(value[None], (devices, *value.shape)), axis, 0, 0, tiled=True
    )


def collect(value, axis, dim):
    return laid_out(sent_to_all(value, axis), dim)


def gathered_once(value, axis):
    leaves = jax.tree.leaves(value)
    sequence = sorted(range(len(leaves)), key=lambda k: -leaves[k].size)
    width = (1, *leaves[sequence[0]].shape)[-1]
    lines = [
        jnp.pad(leaves[k].reshape(-1), (0, -leaves[k].size % width)).reshape(-1, width)
        for k in sequence
    ]
    both, at, found = (sent_to_all(jnp.concatenate(lines), axis), 0, {})
    for k, line in zip(sequence, lines):
        slab = both[:, at : at + len(line)].reshape(len(both), -1)
        found[k] = slab[:, : leaves[k].size].reshape(-1, *leaves[k].shape)
        at += len(line)
    numbers = iter(range(len(leaves)))
    return jax.tree.map(lambda _: found[next(numbers)], value)


def folded_in_pairs(pieces, combine):
    while len(jax.tree.leaves(pieces)[0]) > 1:
        pieces = jax.vmap(combine)(
            *(jax.tree.map(lambda part: part[side::2], pieces) for side in (0, 1))
        )
    return jax.tree.map(lambda part: part[0], pieces)


def joined_all(value, axis, combine):
    pieces = gathered_once(value, axis)
    return folded_in_pairs(pieces, combine)


def split_up(value, dim, devices):
    before, after = (value.shape[:dim], value.shape[dim + 1 :])
    return jnp.moveaxis(value.reshape(*before, devices, -1, *after), dim, 0)


def sum_at_owner(value, axis, dim):
    devices = lax.axis_size(axis)
    blocks = lax.all_to_all(split_up(value, dim, devices), axis, 0, 0, tiled=True)
    return jnp.sum(blocks, axis=0)


def scatter_pairs(value, chips, core, dim):
    sizes = (lax.axis_size(chips), lax.axis_size(core))
    blocks = split_up(value, dim, sizes[0] * sizes[1])
    inside = blocks.shape[1:]
    blocks = blocks.reshape(*sizes, *inside).swapaxes(0, 1).reshape(-1, *inside)
    blocks = lax.psum_scatter(blocks, core, scatter_dimension=0, tiled=True)
    return lax.psum_scatter(blocks, chips, scatter_dimension=0, tiled=True)[0]


def combine_rows(earlier, later):
    highest = jnp.maximum(earlier[0], later[0])
    exp_total = earlier[1] * jnp.exp(earlier[0] - highest) + later[1] * jnp.exp(later[0] - highest)
    return (highest, exp_total, earlier[2] + later[2])


def row_scores(query_rows, passage_rows):
    return (
        lax.dot_general(
            query_rows, passage_rows, (((1,), (1,)), ((), ())), preferred_element_type=jnp.float32
        )
        * logit_scale
    )


def local_stats(scores, onehot):
    highest = jnp.max(scores, axis=1)
    exp_total = jnp.sum(jnp.exp(scores - highest[:, None]), axis=1)
    positive_score = jnp.sum(onehot * scores, axis=1)
    return (highest, exp_total, positive_score)


def body(queries, passages, positives):
    row_count = queries.shape[0]
    groups = lax.axis_size("sub")
    member = lax.axis_index("sub")
    query_half = queries.astype(jnp.bfloat16)
    passage_half = passages.astype(jnp.bfloat16)
    query_rows, row_targets = (collect(query_half, "sub", 0), collect(positives, "sub", 0))
    width_cols = row_count * lax.axis_size(DP)
    passage_rows = lax.all_gather(passage_half, DP, axis=0, tiled=True)
    scores = row_scores(query_rows, passage_rows)
    column = jnp.arange(width_cols, dtype=jnp.int32)
    column_ids = (column // row_count * groups + member) * row_count + column % row_count
    onehot = (column_ids[None, :] == row_targets[:, None]).astype(jnp.float32)
    highest, exp_total, positive_score = local_stats(scores, onehot)
    highest, exp_total, positive_score = joined_all(
        (highest, exp_total, positive_score), "sub", combine_rows
    )
    log_norm = highest + jnp.log(exp_total)
    losses = lax.dynamic_slice_in_dim(log_norm - positive_score, member * row_count, row_count)
    weights = ((jnp.exp(scores - log_norm[:, None]) - onehot) * logit_scale).astype(jnp.bfloat16)
    query_terms = jnp.dot(weights, passage_rows, preferred_element_type=jnp.float32)
    query_grads = sum_at_owner(query_terms, "sub", 0)
    passage_grads = scatter_pairs(
        lax.dot_general(
            weights, query_rows, (((0,), (0,)), ((), ())), preferred_element_type=jnp.float32
        ),
        ("dp_0", "dp_1", "dp_2"),
        "dp_3",
        0,
    )
    return (losses, query_grads, passage_grads)


def solution(mesh):
    torus = Mesh(
        mesh.devices.reshape(4, 2, 4, 2, mesh.shape["sub"]), ("dp_0", "dp_1", "dp_2", "dp_3", "sub")
    )
    placed = (P(DP_SUB, None), P(DP_SUB, None), P(DP_SUB))
    return jax.shard_map(
        body,
        mesh=torus,
        in_specs=placed,
        out_specs=(P(DP_SUB), P(DP_SUB, None), P(DP_SUB, None)),
        check_vma=False,
    )
```

profile of v0, /device:TPU:64, one launch (start us, length us, event | category | flops | bytes accessed | tf_op | source)
XLA Modules:
  0.0 401.1 jit_solution(4751008625709761402)
XLA Ops:
  7.2 0.0 all-gather.2.cloned.1.call-start
  7.2 1.6 convert_element_type.19
  8.8 0.0 all-gather.2.cloned.1.call-update
  8.9 1.2 broadcast_in_dim.7
  10.1 8.1 %all-to-all-start.1 = ((s32[4,1,64]{2,1,0:T(1,128)}), s32[4,1,64]{2,1,0:T(1,128)S(1)}, u32[]{:S(2)}, u32[]{:S(2)}) async-start(s32[4,1,64]{2,1,0:T(1,128)} %broadcast_in_dim.7), calls=%async_computation.1 | async-start | bytes 4096 | tf_op jit(solution)/shard_map/all_to_all | solution.py:20
  18.2 1.0 convert_element_type.18
  19.2 4.3 %all-to-all-done.1 = s32[4,1,64]{2,1,0:T(1,128)S(1)} async-done(((s32[4,1,64]{2,1,0:T(1,128)}), s32[4,1,64]{2,1,0:T(1,128)S(1)}, u32[]{:S(2)}, u32[]{:S(2)}) %all-to-all-start.1) | async-done | bytes 1056 | tf_op jit(solution)/shard_map/all_to_all | solution.py:20
  23.5 0.8 broadcast_in_dim.6
  24.3 5.8 %all-to-all-start = ((bf16[4,64,1024]{2,1,0:T(8,128)(2,1)}), bf16[4,64,1024]{2,1,0:T(8,128)(2,1)S(1)}, u32[]{:S(2)}, u32[]{:S(2)}) async-start(bf16[4,64,1024]{2,1,0:T(8,128)(2,1)} %broadcast_in_dim.6), calls=%async_computation | async-start | bytes 1048576 | tf_op jit(solution)/shard_map/all_to_all | solution.py:20
  30.1 0.0 reduce-scatter.3.cloned.1.call-start
  30.1 0.5 broadcast.96
  30.6 0.7 reduce.3
  31.3 0.1 eq.25
  31.4 17.7 %all-to-all-done = bf16[4,64,1024]{2,1,0:T(8,128)(2,1)S(1)} async-done(((bf16[4,64,1024]{2,1,0:T(8,128)(2,1)}), bf16[4,64,1024]{2,1,0:T(8,128)(2,1)S(1)}, u32[]{:S(2)}, u32[]{:S(2)}) %all-to-all-start) | async-done | bytes 524320 | tf_op jit(solution)/shard_map/all_to_all | solution.py:20
  49.1 79.8 %all-gather.2.cloned.1.call-done = bf16[4096,1024]{1,0:T(8,128)(2,1)} async-done(((bf16[64,1024]{1,0:T(8,128)(2,1)}), bf16[4096,1024]{1,0:T(8,128)(2,1)}) %all-gather.2.cloned.1.call-update) | async-done | bytes 8388624 | tf_op jit(solution)/shard_map/all_gather | solution.py:109
  128.9 5.9 %fusion.27 = (f32[256]{0:T(256)S(1)}, f32[256,4096]{1,0:T(8,128)S(1)}) fusion(bf16[256,1024]{1,0:T(8,128)(2,1)S(1)} %bitcast.36, bf16[4096,1024]{1,0:T(8,128)(2,1)} %all-gather.2.cloned.1.call-done), kind=kOutput, calls=%fused_computation.47 | convolution fusion | flops 2149580544 | bytes 13108224 | tf_op jit(solution)/shard_map/dot_general | solution.py:87
  134.8 0.0 copy-start
  134.8 2.0 copy-done
  136.9 1.1 exponential_reduce_fusion
  138.0 11.9 %all_to_all.21 = f32[4,3,256]{2,1,0:T(4,128)S(1)} all-to-all(f32[4,3,256]{2,1,0:T(4,128)S(1)} %broadcast_in_dim.8), channel_id=1, replica_groups=mesh['dp_0'=4,'dp_1'=2,'dp_2'=4,'dp_3'=2,'sub'=4] {'sub'}, dimensions={0} | all-to-all | bytes 24576 | tf_op jit(solution)/shard_map/all_to_all | solution.py:20
  150.0 4.7 %fusion.5 = bf16[4096,256]{0,1:T(8,128)(2,1)} fusion(f32[256,4096]{1,0:T(8,128)} %copy-done, s32[4096]{0:T(1024)S(1)} %fusion.21, f32[256]{0:T(256)S(1)} %bitcast.40, s32[256]{0:T(256)S(1)} %eq.25), kind=kLoop, calls=%fused_computation.10 | loop fusion | flops 6291456 | bytes 6309888 | tf_op jit(solution)/shard_map/convert_element_type | solution.py:120
  154.8 3.3 copy.9
  158.0 2.3 convolution_bitcast_fusion
  160.4 6.0 %copy.10 = f32[2,32,64,1024]{3,2,1,0:T(8,128)} copy(f32[2,32,64,1024]{3,2,0,1:T(8,128)S(1)} %convolution_bitcast_fusion) | data formatting | bytes 33554432 | tf_op jit(solution)/shard_map/transpose | solution.py:74
  166.4 0.0 reduce-scatter.3.cloned.1.call-update
  166.5 0.0 reduce-scatter.5.cloned.1.call-start
  166.5 27.7 %reduce-scatter.3.cloned.1.call-done = f32[32,64,1024]{2,1,0:T(8,128)} async-done(((f32[64,64,1024]{2,1,0:T(8,128)}), f32[32,64,1024]{2,1,0:T(8,128)}) %reduce-scatter.3.cloned.1.call-update) | async-done | bytes 8388624 | tf_op jit(solution)/shard_map/reduce_scatter | solution.py:75
  194.3 0.0 reduce-scatter.5.cloned.1.call-update
  194.3 8.1 %fusion.6 = f32[256,1024]{1,0:T(8,128)} fusion(bf16[4096,1024]{1,0:T(8,128)(2,1)} %all-gather.2.cloned.1.call-done, f32[256,4096]{1,0:T(8,128)} %copy-done, f32[256]{0:T(256)S(1)} %bitcast.41, s32[4096]{0:T(1024)S(1)} %fusion.21, s32[256]{0:T(256)S(1)} %eq.25), kind=kOutput, calls=%fused_computation.13 | convolution fusion | flops 2153775104 | bytes 13649920 | tf_op jit(solution)/shard_map/dot_general | solution.py:121
  202.4 7.4 %all-to-all-start.3 = ((f32[4,64,1024]{2,1,0:T(8,128)}), f32[4,64,1024]{2,1,0:T(8,128)S(1)}, u32[]{:S(2)}, u32[]{:S(2)}) async-start(f32[4,64,1024]{2,1,0:T(8,128)} %bitcast.7), calls=%async_computation.3 | async-start | bytes 2097152 | tf_op jit(solution)/shard_map/all_to_all | solution.py:66
  209.8 0.6 dynamic_slice.3
  210.4 35.8 %all-to-all-done.3 = f32[4,64,1024]{2,1,0:T(8,128)S(1)} async-done(((f32[4,64,1024]{2,1,0:T(8,128)}), f32[4,64,1024]{2,1,0:T(8,128)S(1)}, u32[]{:S(2)}, u32[]{:S(2)}) %all-to-all-start.3) | async-done | bytes 1048608 | tf_op jit(solution)/shard_map/all_to_all | solution.py:66
  246.2 0.8 reduce_sum.29
  247.0 147.6 %reduce-scatter.5.cloned.1.call-done = f32[1,64,1024]{2,1,0:T(8,128)} async-done(((f32[32,64,1024]{2,1,0:T(8,128)}), f32[1,64,1024]{2,1,0:T(8,128)}) %reduce-scatter.5.cloned.1.call-update) | async-done | bytes 262160 | tf_op jit(solution)/shard_map/reduce_scatter | solution.py:76
  (17 shorter events, 0.3 us)
Async XLA Ops:
  7.2 121.8 %all-gather.2.cloned.1.call-start = ((), (), s32[]{:S(2)}) async-start(), calls=%async_computation.6 | async-start | bytes 8519680 | tf_op jit(solution)/shard_map/all_gather | solution.py:109
  10.1 13.4 %all-to-all-start.1 = ((s32[4,1,64]{2,1,0:T(1,128)}), s32[4,1,64]{2,1,0:T(1,128)S(1)}, u32[]{:S(2)}, u32[]{:S(2)}) async-start(s32[4,1,64]{2,1,0:T(1,128)} %broadcast_in_dim.7), calls=%async_computation.1 | async-start | bytes 4096 | tf_op jit(solution)/shard_map/all_to_all | solution.py:20
  24.3 24.8 %all-to-all-start = ((bf16[4,64,1024]{2,1,0:T(8,128)(2,1)}), bf16[4,64,1024]{2,1,0:T(8,128)(2,1)S(1)}, u32[]{:S(2)}, u32[]{:S(2)}) async-start(bf16[4,64,1024]{2,1,0:T(8,128)(2,1)} %broadcast_in_dim.6), calls=%async_computation | async-start | bytes 1048576 | tf_op jit(solution)/shard_map/all_to_all | solution.py:20
  30.1 164.1 %reduce-scatter.3.cloned.1.call-start = ((), (), s32[]{:S(2)}) async-start(), calls=%async_computation.7 | async-start | bytes 25165824 | tf_op jit(solution)/shard_map/reduce_scatter | solution.py:75
  134.8 2.0 copy-start
  166.5 228.1 %reduce-scatter.5.cloned.1.call-start = ((), (), s32[]{:S(2)}) async-start(), calls=%async_computation.8 | async-start | bytes 8650752 | tf_op jit(solution)/shard_map/reduce_scatter | solution.py:76
  202.4 43.8 %all-to-all-start.3 = ((f32[4,64,1024]{2,1,0:T(8,128)}), f32[4,64,1024]{2,1,0:T(8,128)S(1)}, u32[]{:S(2)}, u32[]{:S(2)}) async-start(f32[4,64,1024]{2,1,0:T(8,128)} %bitcast.7), calls=%async_computation.3 | async-start | bytes 2097152 | tf_op jit(solution)/shard_map/all_to_all | solution.py:66
Sparse Core Ops, SparseCore 0:
  10.4 118.4 all-gather.1
  166.6 27.6 reduce-scatter.2
  197.4 197.0 reduce-scatter.4
where the time goes:
time: 402 us; the launch traced here: 401 us
  waiting for transfers between devices  313 us (78%)
  starting transfers between devices  21.4 us (5%)
  matrix products  16.3 us (4%)
  local copies, waits for them, and re-layouts  14.8 us (4%)
  between operations  13.8 us (3%)
  blocking collectives  11.9 us (3%)
  other arithmetic  9.91 us (2%)
    reduce_scatter x1, waiting for transfers between devices, scatter_pairs(): return lax.psum_scatter(blocks, chips, scatter_dimension=0, tiled=True)[0]  148 us
    all_gather x1, waiting for transfers between devices, body(): passage_rows = lax.all_gather(passage_half, DP, axis=0, tiled=True)  79.8 us
    all_to_all x1, waiting for transfers between devices, sum_at_owner(): lax.all_to_all(split_up(value, dim, devices), axis, 0, 0, tiled=True)  35.8 us
    reduce_scatter x1, waiting for transfers between devices, scatter_pairs(): blocks = lax.psum_scatter(blocks, core, scatter_dimension=0, tiled=True)  27.7 us
    all_to_all x2, waiting for transfers between devices, sent_to_all(): lax.all_to_all(jnp.broadcast_to(value[None], (devices, *value.shape)), ax...  22 us
    all_to_all x2, starting transfers between devices, sent_to_all(): lax.all_to_all(jnp.broadcast_to(value[None], (devices, *value.shape)), ax...  13.9 us
    all_to_all x1, blocking collectives, sent_to_all(): lax.all_to_all(jnp.broadcast_to(value[None], (devices, *value.shape)), ax...  11.9 us
    dot_general x1, matrix products, body(): jnp.dot(weights, passage_rows, preferred_element_type=jnp.float32)  8.11 us
  transfers between devices with their start and end apart: 6, of which 6 were waited for; matrix products, arithmetic and copies ran while one was open for 3% of the time, Pallas kernels for 0%

commit v1 on v0

--- a/solution.py
+++ b/solution.py
@@ -106,7 +106,10 @@
     passage_half = passages.astype(jnp.bfloat16)
     query_rows, row_targets = (collect(query_half, "sub", 0), collect(positives, "sub", 0))
     width_cols = row_count * lax.axis_size(DP)
-    passage_rows = lax.all_gather(passage_half, DP, axis=0, tiled=True)
+    size = lax.axis_size(DP)
+    parts = jnp.stack([passage_half for _ in range(size)])
+    parts = lax.all_to_all(parts, DP, split_axis=0, concat_axis=0)
+    passage_rows = jnp.concatenate(parts, axis=0)
     scores = row_scores(query_rows, passage_rows)
     column = jnp.arange(width_cols, dtype=jnp.int32)
     column_ids = (column // row_count * groups + member) * row_count + column % row_count

time: 402 us -> 434 us (1.080)
  waiting for transfers between devices: 313 us -> 333 us
  starting transfers between devices: 21.4 us -> 29.7 us
    all_to_all x0 -> x1, waiting for transfers between devices: none -> 105 us  [body(): parts = lax.all_to_all(parts, DP, split_axis=0, concat_axis=0)]
    all_gather x1 -> x0, waiting for transfers between devices: 79.8 us -> none  [body(): passage_rows = lax.all_gather(passage_half, DP, axis=0, tiled=True)]
    all_to_all x0 -> x1, starting transfers between devices: none -> 8.2 us  [body(): parts = lax.all_to_all(parts, DP, split_axis=0, concat_axis=0)]
    all_to_all x2, waiting for transfers between devices: 22 us -> 17.3 us  [sent_to_all(): lax.all_to_all(jnp.broadcast_to(value[None], (devices, *value.shape)), ax...]
where the time goes in v1:
time: 434 us; the launch traced here: 433 us
  waiting for transfers between devices  333 us (77%)
  starting transfers between devices  29.7 us (7%)
  local copies, waits for them, and re-layouts  19.1 us (4%)
  matrix products  14.9 us (3%)
  between operations  14.1 us (3%)
  other arithmetic  12.6 us (3%)
  blocking collectives  9.95 us (2%)
    reduce_scatter x1, waiting for transfers between devices, scatter_pairs(): return lax.psum_scatter(blocks, chips, scatter_dimension=0, tiled=True)[0]  146 us
    all_to_all x1, waiting for transfers between devices, body(): parts = lax.all_to_all(parts, DP, split_axis=0, concat_axis=0)  105 us
    all_to_all x1, waiting for transfers between devices, sum_at_owner(): lax.all_to_all(split_up(value, dim, devices), axis, 0, 0, tiled=True)  34.9 us
    reduce_scatter x1, waiting for transfers between devices, scatter_pairs(): blocks = lax.psum_scatter(blocks, core, scatter_dimension=0, tiled=True)  29.5 us
    all_to_all x2, waiting for transfers between devices, sent_to_all(): lax.all_to_all(jnp.broadcast_to(value[None], (devices, *value.shape)), ax...  17.3 us
    all_to_all x2, starting transfers between devices, sent_to_all(): lax.all_to_all(jnp.broadcast_to(value[None], (devices, *value.shape)), ax...  13.9 us
    all_to_all x1, blocking collectives, sent_to_all(): lax.all_to_all(jnp.broadcast_to(value[None], (devices, *value.shape)), ax...  9.95 us
  transfers between devices with their start and end apart: 6, of which 6 were waited for; matrix products, arithmetic and copies ran while one was open for 3% of the time, Pallas kernels for 0%

profile of v1, /device:TPU:64, one launch (start us, length us, event | category | flops | bytes accessed | tf_op | source)
XLA Modules:
  0.0 433.0 jit_solution(215009586957323386)
XLA Ops:
  7.2 1.2 broadcast_in_dim.7
  8.4 8.1 %all-to-all-start.2 = ((s32[4,1,64]{2,1,0:T(1,128)}), s32[4,1,64]{2,1,0:T(1,128)S(1)}, u32[]{:S(2)}, u32[]{:S(2)}) async-start(s32[4,1,64]{2,1,0:T(1,128)} %broadcast_in_dim.7), calls=%async_computation.2 | async-start | bytes 4096 | tf_op jit(solution)/shard_map/all_to_all | solution.py:20
  16.5 1.0 convert_element_type.18
  17.5 4.3 all-to-all-done.2
  21.8 0.8 broadcast_in_dim.6
  22.6 5.8 %all-to-all-start = ((bf16[4,64,1024]{2,1,0:T(8,128)(2,1)}), bf16[4,64,1024]{2,1,0:T(8,128)(2,1)S(1)}, u32[]{:S(2)}, u32[]{:S(2)}) async-start(bf16[4,64,1024]{2,1,0:T(8,128)(2,1)} %broadcast_in_dim.6), calls=%async_computation | async-start | bytes 1048576 | tf_op jit(solution)/shard_map/all_to_all | solution.py:20
  28.4 1.0 convert_element_type.19
  29.4 13.0 %all-to-all-done = bf16[4,64,1024]{2,1,0:T(8,128)(2,1)S(1)} async-done(((bf16[4,64,1024]{2,1,0:T(8,128)(2,1)}), bf16[4,64,1024]{2,1,0:T(8,128)(2,1)S(1)}, u32[]{:S(2)}, u32[]{:S(2)}) %all-to-all-start) | async-done | bytes 524320 | tf_op jit(solution)/shard_map/all_to_all | solution.py:20
  42.4 4.3 stack.2
  46.7 8.2 %all-to-all-start.1 = ((bf16[64,64,1024]{2,1,0:T(8,128)(2,1)}), bf16[64,64,1024]{2,1,0:T(8,128)(2,1)}, u32[]{:S(2)}, u32[]{:S(2)}) async-start(bf16[64,64,1024]{2,1,0:T(8,128)(2,1)} %stack.2), calls=%async_computation.1 | async-start | bytes 16777216 | tf_op jit(solution)/shard_map/all_to_all | solution.py:111
  54.9 0.0 reduce-scatter.3.cloned.1.call-start
  55.0 0.5 broadcast.95
  55.5 0.7 reduce.3
  56.2 0.1 eq.25
  56.2 105.1 %all-to-all-done.1 = bf16[64,64,1024]{2,1,0:T(8,128)(2,1)} async-done(((bf16[64,64,1024]{2,1,0:T(8,128)(2,1)}), bf16[64,64,1024]{2,1,0:T(8,128)(2,1)}, u32[]{:S(2)}, u32[]{:S(2)}) %all-to-all-start.1) | async-done | bytes 8388640 | tf_op jit(solution)/shard_map/all_to_all | solution.py:111
  161.3 5.8 %fusion.20 = (f32[256]{0:T(256)S(1)}, f32[256,4096]{1,0:T(8,128)S(1)}) fusion(bf16[256,1024]{1,0:T(8,128)(2,1)S(1)} %bitcast.40, bf16[4096,1024]{1,0:T(8,128)(2,1)} %bitcast.1), kind=kOutput, calls=%fused_computation.41 | convolution fusion | flops 2149580544 | bytes 13108224 | tf_op jit(solution)/shard_map/dot_general | solution.py:87
  167.2 0.0 copy-start
  167.2 2.0 copy-done
  169.2 1.1 exponential_reduce_fusion
  170.3 9.9 %all_to_all.26 = f32[4,3,256]{2,1,0:T(4,128)S(1)} all-to-all(f32[4,3,256]{2,1,0:T(4,128)S(1)} %broadcast_in_dim.8), channel_id=1, replica_groups=mesh['dp_0'=4,'dp_1'=2,'dp_2'=4,'dp_3'=2,'sub'=4] {'sub'}, dimensions={0} | all-to-all | bytes 24576 | tf_op jit(solution)/shard_map/all_to_all | solution.py:20
  180.5 4.7 %fusion.5 = bf16[4096,256]{0,1:T(8,128)(2,1)} fusion(f32[256,4096]{1,0:T(8,128)} %copy-done, s32[4096]{0:T(1024)S(1)} %fusion.15, f32[256]{0:T(256)S(1)} %bitcast.43, s32[256]{0:T(256)S(1)} %eq.25), kind=kLoop, calls=%fused_computation.10 | loop fusion | flops 6291456 | bytes 6309888 | tf_op jit(solution)/shard_map/convert_element_type | solution.py:123
  185.2 3.3 copy.9
  188.4 2.3 convolution_bitcast_fusion
  190.8 6.0 %copy.10 = f32[2,32,64,1024]{3,2,1,0:T(8,128)} copy(f32[2,32,64,1024]{3,2,0,1:T(8,128)S(1)} %convolution_bitcast_fusion) | data formatting | bytes 33554432 | tf_op jit(solution)/shard_map/transpose | solution.py:74
  196.8 0.0 reduce-scatter.3.cloned.1.call-update
  196.9 0.2 reduce-scatter.5.cloned.1.call-start
  197.1 29.5 %reduce-scatter.3.cloned.1.call-done = f32[32,64,1024]{2,1,0:T(8,128)} async-done(((f32[64,64,1024]{2,1,0:T(8,128)}), f32[32,64,1024]{2,1,0:T(8,128)}) %reduce-scatter.3.cloned.1.call-update) | async-done | bytes 8388624 | tf_op jit(solution)/shard_map/reduce_scatter | solution.py:75
  226.6 0.0 reduce-scatter.5.cloned.1.call-update
  226.6 3.3 fusion.3
  229.9 6.7 %fusion.21 = f32[4,64,1024]{2,1,0:T(8,128)} fusion(bf16[4,64,4096]{2,1,0:T(8,128)(2,1)S(1)} %bitcast.42, bf16[4096,1024,1]{1,0,2:T(8,128)(2,1)} %bitcast.9), kind=kOutput, calls=%fused_computation.42 | convolution fusion | flops 2147483648 | bytes 11534336 | tf_op jit(solution)/shard_map/dot_general | solution.py:124
  236.6 7.4 %all-to-all-start.4 = ((f32[4,64,1024]{2,1,0:T(8,128)}), f32[4,64,1024]{2,1,0:T(8,128)S(1)}, u32[]{:S(2)}, u32[]{:S(2)}) async-start(f32[4,64,1024]{2,1,0:T(8,128)} %fusion.21), calls=%async_computation.4 | async-start | bytes 2097152 | tf_op jit(solution)/shard_map/all_to_all | solution.py:66
  244.0 0.6 dynamic_slice.3
  244.6 34.9 %all-to-all-done.4 = f32[4,64,1024]{2,1,0:T(8,128)S(1)} async-done(((f32[4,64,1024]{2,1,0:T(8,128)}), f32[4,64,1024]{2,1,0:T(8,128)S(1)}, u32[]{:S(2)}, u32[]{:S(2)}) %all-to-all-start.4) | async-done | bytes 1048608 | tf_op jit(solution)/shard_map/all_to_all | solution.py:66
  279.5 0.8 reduce_sum.29
  280.3 145.8 %reduce-scatter.5.cloned.1.call-done = f32[1,64,1024]{2,1,0:T(8,128)} async-done(((f32[32,64,1024]{2,1,0:T(8,128)}), f32[1,64,1024]{2,1,0:T(8,128)}) %reduce-scatter.5.cloned.1.call-update) | async-done | bytes 262160 | tf_op jit(solution)/shard_map/reduce_scatter | solution.py:76
  (17 shorter events, 0.3 us)
Async XLA Ops:
  8.4 13.4 %all-to-all-start.2 = ((s32[4,1,64]{2,1,0:T(1,128)}), s32[4,1,64]{2,1,0:T(1,128)S(1)}, u32[]{:S(2)}, u32[]{:S(2)}) async-start(s32[4,1,64]{2,1,0:T(1,128)} %broadcast_in_dim.7), calls=%async_computation.2 | async-start | bytes 4096 | tf_op jit(solution)/shard_map/all_to_all | solution.py:20
  22.6 19.8 %all-to-all-start = ((bf16[4,64,1024]{2,1,0:T(8,128)(2,1)}), bf16[4,64,1024]{2,1,0:T(8,128)(2,1)S(1)}, u32[]{:S(2)}, u32[]{:S(2)}) async-start(bf16[4,64,1024]{2,1,0:T(8,128)(2,1)} %broadcast_in_dim.6), calls=%async_computation | async-start | bytes 1048576 | tf_op jit(solution)/shard_map/all_to_all | solution.py:20
  46.7 114.6 %all-to-all-start.1 = ((bf16[64,64,1024]{2,1,0:T(8,128)(2,1)}), bf16[64,64,1024]{2,1,0:T(8,128)(2,1)}, u32[]{:S(2)}, u32[]{:S(2)}) async-start(bf16[64,64,1024]{2,1,0:T(8,128)(2,1)} %stack.2), calls=%async_computation.1 | async-start | bytes 16777216 | tf_op jit(solution)/shard_map/all_to_all | solution.py:111
  54.9 171.6 %reduce-scatter.3.cloned.1.call-start = ((), (), s32[]{:S(2)}) async-start(), calls=%async_computation.7 | async-start | bytes 25165824 | tf_op jit(solution)/shard_map/reduce_scatter | solution.py:75
  167.2 2.1 copy-start
  196.9 229.3 %reduce-scatter.5.cloned.1.call-start = ((), (), s32[]{:S(2)}) async-start(), calls=%async_computation.8 | async-start | bytes 8650752 | tf_op jit(solution)/shard_map/reduce_scatter | solution.py:76
  236.6 42.9 %all-to-all-start.4 = ((f32[4,64,1024]{2,1,0:T(8,128)}), f32[4,64,1024]{2,1,0:T(8,128)S(1)}, u32[]{:S(2)}, u32[]{:S(2)}) async-start(f32[4,64,1024]{2,1,0:T(8,128)} %fusion.21), calls=%async_computation.4 | async-start | bytes 2097152 | tf_op jit(solution)/shard_map/all_to_all | solution.py:66
Sparse Core Ops, SparseCore 0:
  197.0 29.5 reduce-scatter.2
  229.7 196.4 reduce-scatter.4
